TPU v7x, 256 devices: a whole 4x4x8 slice. The times are simulated.
256 devices in a mesh: row: 8 (over x, z_lo), col: 32 (over z_hi, y, core).
Axes of the slice: x: 4, y: 4, z: 8 (z_hi: 4, z_lo: 2; z = z_hi * 2 + z_lo), core: 2. Of those that a mesh axis runs over, the one named last changes fastest.
Arguments:
- tile_values: float32 [8, 32, 64, 128, 128], P('row', 'col'), may hold values from -0.15625 to 0.15625
- tile_rows: int32 [8, 32, 64], P('row', 'col'), may hold values from 0 to 159, as said below
- tile_cols: int32 [8, 32, 64], P('row', 'col'), may hold values from 0 to 23
- x_start: float32 [768, 128], P('col', 'row'), may hold values from -6 to 6
- z_start: float32 [1280, 128], P('row'), may hold values from -6 to 6
- y_start: float32 [1280, 128], P('row'), may hold values from -3 to 3
- lower_bound: float32 [1280, 128], P('row'), may hold values from -1.5 to -0.1
- upper_bound: float32 [1280, 128], P('row'), may hold values from 0.1 to 1.5
- cost_diag: float32 [768, 128], P('col', 'row'), may hold values from 0.1 to 10
- linear: float32 [768, 128], P('col', 'row'), may hold values from -6 to 6
- penalty: float32 [1], replicated, may hold values from 0.3 to 3
- proximal: float32 [1], replicated, may hold values from 0.1 to 1
- relaxation: float32 [1], replicated, may hold values from 1.2 to 1.8
Outputs:
- x_next: float32 [768, 128], P('col', 'row')
- z_next: float32 [1280, 128], P('row')
- y_next: float32 [1280, 128], P('row')
Inputs may be any that keep to these rules, and one draw needn't show every extreme that they name: On each device the 64 pairs (tile_rows, tile_cols) are distinct.
All inputs are finite; a program needn't handle non-finite values.
Results may differ from a plain program's by a relative error of at most 0.0002.
Values sent between devices are 32-bit elements; how exact they have to be, the bound alone decides.
A program may use at most 64 MiB of HBM per device.

v0:
```python
import jax
import jax.numpy as jnp
from jax import lax
from jax.sharding import PartitionSpec as P

ADMM_ITERS = 2
HIGH = lax.Precision.HIGHEST


def total_of_pieces(array, axis):
    return lax.all_gather(array, axis).sum(0)


def from_everyone(array, axis):
    copies = jnp.broadcast_to(array, (lax.axis_size(axis), *array.shape))
    return lax.all_to_all(copies, axis, split_axis=0, concat_axis=0, tiled=True)


def of_everyone(array, axis):
    everything = from_everyone(array, axis)
    return jnp.sum(everything, axis=0)


def turned_gather(arrays, axis, dims):
    turned = [jnp.moveaxis(a, dim, 0) for a, dim in zip(arrays, dims)]
    widths = [t[0].size for t in turned]
    both = jnp.concatenate([t.reshape(-1, w) for t, w in zip(turned, widths)], axis=1)
    out = lax.all_gather(both, axis, axis=0, tiled=True)
    parts = jnp.split(out, [sum(widths[:k]) for k in range(1, len(widths))], axis=1)
    return tuple(
        (
            jnp.moveaxis(b.reshape(-1, *t.shape[1:]), 0, dim)
            for b, t, dim in zip(parts, turned, dims)
        )
    )


def shards(
    tile_values,
    tile_rows,
    tile_cols,
    x_start,
    z_start,
    y_start,
    lower_bound,
    upper_bound,
    cost_diag,
    linear,
    penalty,
    proximal,
    relaxation,
):
    order_size = tile_values.shape[3]
    flat_tiles = tile_values.reshape(-1, order_size, order_size)
    row_index = tile_rows.reshape(-1)
    col_index = tile_cols.reshape(-1)
    count_tiles = row_index.shape[0]
    block_rows = z_start.shape[0]
    block_cols = x_start.shape[0]
    row_table = (
        lax.broadcasted_iota(jnp.int32, (block_rows, count_tiles), 0) == row_index[None, :]
    ).astype(jnp.float32)
    col_table = (
        lax.broadcasted_iota(jnp.int32, (block_cols, count_tiles), 0) == col_index[None, :]
    ).astype(jnp.float32)
    rho_value = penalty[0]
    sigma_value = proximal[0]
    relax_value = relaxation[0]
    empty_rows = jnp.zeros((block_rows, order_size), jnp.float32)

    def forward_terms(segment):
        piece_width = segment.shape[1]
        picked = jnp.take(segment, col_index, axis=0)
        products = jnp.einsum("kij,kj->ki", flat_tiles, picked, precision=HIGH)
        return jnp.dot(row_table, products, precision=HIGH)

    def apply_forward(vector):
        local_part = forward_terms(vector)
        return total_of_pieces(local_part, "col")

    def apply_backward(weights_rows):
        picked = jnp.take(weights_rows, row_index, axis=0)
        products = jnp.einsum("kij,ki->kj", flat_tiles, picked, precision=HIGH)
        local_part = jnp.dot(col_table, products, precision=HIGH)
        return of_everyone(local_part, "row")

    def global_totals(values):
        stacked = jnp.stack([jnp.sum(value) for value in values])
        return of_everyone(stacked, "col")

    x_now, diag_now, linear_now = turned_gather((x_start, cost_diag, linear), "row", (1, 1, 1))
    z_now, y_now = (z_start, y_start)
    image_now = empty_rows
    for outer_round in range(ADMM_ITERS):
        if outer_round == 0:
            image_now = apply_forward(x_now)
        target = rho_value * z_now - y_now - rho_value * image_now
        residual = -linear_now - diag_now * x_now + apply_backward(target)
        guess = x_now
        direction = residual
        image_sum = image_now
        norm_now = jnp.float32(1.0)
        norm_now = global_totals([residual * residual])[0]
        pushed = apply_forward(direction)
        applied = (diag_now + sigma_value) * direction + rho_value * apply_backward(pushed)
        curvature = global_totals([direction * applied])[0]
        step_length = norm_now / curvature
        guess = guess + step_length * direction
        image_sum = image_sum + step_length * pushed
        residual = residual - step_length * applied
        image_now = relax_value * image_sum + (1.0 - relax_value) * image_now
        x_now = relax_value * guess + (1.0 - relax_value) * x_now
        mixed = relax_value * image_sum + (1.0 - relax_value) * z_now
        z_fresh = jnp.minimum(jnp.maximum(mixed + y_now / rho_value, lower_bound), upper_bound)
        y_now = y_now + rho_value * (mixed - z_fresh)
        z_now = z_fresh
    piece_width = x_start.shape[1]
    x_now = lax.dynamic_slice_in_dim(x_now, lax.axis_index("row") * piece_width, piece_width, 1)
    return (x_now, z_now, y_now)


def solution(mesh):
    placed = (
        P("row", "col", None, None, None),
        P("row", "col", None),
        P("row", "col", None),
        P("col", "row"),
        P("row", None),
        P("row", None),
        P("row", None),
        P("row", None),
        P("col", "row"),
        P("col", "row"),
        P(),
        P(),
        P(),
    )
    return jax.shard_map(
        shards,
        mesh=mesh,
        in_specs=placed,
        out_specs=(P("col", "row"), P("row", None), P("row", None)),
        check_vma=False,
    )
```

profile of v0, /device:TPU:1, one launch (start us, length us, event | category | flops | bytes accessed | tf_op | source)
XLA Modules:
  0.0 375.3 jit_solution(2561918909377386901)
XLA Ops:
  9.4 23.0 %all_gather.21 = f32[128,72]{1,0:T(8,128)S(1)} all-gather(f32[16,72]{1,0:T(8,128)S(1)} %pad_maximum_fusion), channel_id=1, replica_groups=mesh['row'=8,'col'=32] {'row'}, dimensions={0}, use_global_device_ids=true | all-gather | bytes 41472 | tf_op jit(solution)/shard_map/all_gather | solution.py:28
  33.3 8.3 %fusion.12 = f32[64,1,128]{2,1,0:T(1,128)S(1)} fusion(f32[64,128,1]{1,2,0:T(1,128)S(1)} %bitcast.125, f32[1,1,64,128,128]{4,3,2,1,0:T(8,128)} %param.17), kind=kOutput, calls=%fused_computation.19 | convolution fusion | flops 12582912 | bytes 4259840 | tf_op jit(solution)/shard_map/kij,kj->ki/dot_general | solution.py:74
  43.2 63.6 %all-gather.7.cloned.1.call-done = f32[5120,128]{1,0:T(8,128)} async-done(((f32[160,128]{1,0:T(8,128)}), f32[5120,128]{1,0:T(8,128)}) %all-gather.7.cloned.1.call-update) | async-done | bytes 2621456 | tf_op jit(solution)/shard_map/all_gather | solution.py:11
  106.7 1.9 reduce_sum.135
  109.3 5.3 %fusion.10 = f32[64,1,128]{2,1,0:T(1,128)S(1)} fusion(f32[64,128,1]{1,2,0:T(1,128)S(1)} %bitcast.126, f32[1,1,64,128,128]{4,3,2,1,0:T(8,128)} %param.17), kind=kOutput, calls=%fused_computation.17 | convolution fusion | flops 12582912 | bytes 4259840 | tf_op jit(solution)/shard_map/kij,ki->kj/dot_general | solution.py:83
  115.4 4.0 %all-to-all-start = ((f32[8,24,128]{2,1,0:T(8,128)}), f32[8,24,128]{2,1,0:T(8,128)S(1)}, u32[]{:S(2)}, u32[]{:S(2)}) async-start(f32[8,24,128]{2,1,0:T(8,128)} %broadcast_in_dim.42), calls=%async_computation | async-start | bytes 196608 | tf_op jit(solution)/shard_map/all_to_all | solution.py:16
  119.5 5.2 %all-to-all-done = f32[8,24,128]{2,1,0:T(8,128)S(1)} async-done(((f32[8,24,128]{2,1,0:T(8,128)}), f32[8,24,128]{2,1,0:T(8,128)S(1)}, u32[]{:S(2)}, u32[]{:S(2)}) %all-to-all-start) | async-done | bytes 98336 | tf_op jit(solution)/shard_map/all_to_all | solution.py:16
  125.5 8.3 %fusion.8 = f32[64,1,128]{2,1,0:T(1,128)S(1)} fusion(f32[64,128,1]{1,2,0:T(1,128)S(1)} %bitcast.128, f32[1,1,64,128,128]{4,3,2,1,0:T(8,128)} %param.17), kind=kOutput, calls=%fused_computation.15 | convolution fusion | flops 12582912 | bytes 4259840 | tf_op jit(solution)/shard_map/kij,kj->ki/dot_general | solution.py:74
  134.6 52.7 %all-gather.9.cloned.1.call-done = f32[5120,128]{1,0:T(8,128)} async-done(((f32[160,128]{1,0:T(8,128)}), f32[5120,128]{1,0:T(8,128)}) %all-gather.9.cloned.1.call-update) | async-done | bytes 2621456 | tf_op jit(solution)/shard_map/all_gather | solution.py:11
  187.3 1.9 reduce_sum.139
  189.8 5.3 %fusion.6 = f32[64,1,128]{2,1,0:T(1,128)S(1)} fusion(f32[64,128,1]{1,2,0:T(1,128)S(1)} %bitcast.129, f32[1,1,64,128,128]{4,3,2,1,0:T(8,128)} %param.17), kind=kOutput, calls=%fused_computation.13 | convolution fusion | flops 12582912 | bytes 4259840 | tf_op jit(solution)/shard_map/kij,ki->kj/dot_general | solution.py:83
  195.9 4.0 %all-to-all-start.2 = ((f32[8,24,128]{2,1,0:T(8,128)}), f32[8,24,128]{2,1,0:T(8,128)S(1)}, u32[]{:S(2)}, u32[]{:S(2)}) async-start(f32[8,24,128]{2,1,0:T(8,128)} %broadcast_in_dim.44), calls=%async_computation.2 | async-start | bytes 196608 | tf_op jit(solution)/shard_map/all_to_all | solution.py:16
  200.5 4.7 %all-to-all-done.2 = f32[8,24,128]{2,1,0:T(8,128)S(1)} async-done(((f32[8,24,128]{2,1,0:T(8,128)}), f32[8,24,128]{2,1,0:T(8,128)S(1)}, u32[]{:S(2)}, u32[]{:S(2)}) %all-to-all-start.2) | async-done | bytes 98336 | tf_op jit(solution)/shard_map/all_to_all | solution.py:16
  206.6 16.7 %all_to_all.44 = f32[32,1,1]{2,1,0:T(1,128)S(1)} all-to-all(f32[32,1,1]{2,1,0:T(1,128)S(1)} %broadcast_in_dim.43), channel_id=1, replica_groups=mesh['row'=8,'col'=32] {'col'}, dimensions={0} | all-to-all | bytes 256 | tf_op jit(solution)/shard_map/all_to_all | solution.py:16
  223.2 1.3 broadcast_in_dim.45
  224.5 4.1 %all-to-all-start.3 = ((f32[32,1,1]{2,1,0:T(1,128)}), f32[32,1,1]{2,1,0:T(1,128)S(1)}, u32[]{:S(2)}, u32[]{:S(2)}) async-start(f32[32,1,1]{2,1,0:T(1,128)} %broadcast_in_dim.45), calls=%async_computation.3 | async-start | bytes 32768 | tf_op jit(solution)/shard_map/all_to_all | solution.py:16
  230.2 7.9 %all-to-all-done.3 = f32[32,1,1]{2,1,0:T(1,128)S(1)} async-done(((f32[32,1,1]{2,1,0:T(1,128)}), f32[32,1,1]{2,1,0:T(1,128)S(1)}, u32[]{:S(2)}, u32[]{:S(2)}) %all-to-all-start.3) | async-done | bytes 160 | tf_op jit(solution)/shard_map/all_to_all | solution.py:16
  240.8 5.3 %fusion.4 = f32[64,1,128]{2,1,0:T(1,128)S(1)} fusion(f32[64,128,1]{1,2,0:T(1,128)S(1)} %bitcast.131, f32[1,1,64,128,128]{4,3,2,1,0:T(8,128)} %param.17), kind=kOutput, calls=%fused_computation.11 | convolution fusion | flops 12582912 | bytes 4259840 | tf_op jit(solution)/shard_map/kij,ki->kj/dot_general | solution.py:83
  246.3 7.8 %all_to_all.45 = f32[8,24,128]{2,1,0:T(8,128)S(1)} all-to-all(f32[8,24,128]{2,1,0:T(8,128)S(1)} %broadcast_in_dim.46), channel_id=1, replica_groups=mesh['row'=8,'col'=32] {'row'}, dimensions={0} | all-to-all | bytes 196608 | tf_op jit(solution)/shard_map/all_to_all | solution.py:16
  254.8 8.3 %fusion.2 = f32[64,1,128]{2,1,0:T(1,128)S(1)} fusion(f32[64,128,1]{1,2,0:T(1,128)S(1)} %bitcast.123, f32[1,1,64,128,128]{4,3,2,1,0:T(8,128)} %param.17), kind=kOutput, calls=%fused_computation.9 | convolution fusion | flops 12582912 | bytes 4259840 | tf_op jit(solution)/shard_map/kij,kj->ki/dot_general | solution.py:74
  263.1 0.8 fusion.14
  263.9 49.7 %all-gather.11.cloned.1.call-done = f32[5120,128]{1,0:T(8,128)} async-done(((f32[160,128]{1,0:T(8,128)}), f32[5120,128]{1,0:T(8,128)}) %all-gather.11.cloned.1.call-update) | async-done | bytes 2621456 | tf_op jit(solution)/shard_map/all_gather | solution.py:11
  313.7 1.9 reduce_sum.146
  316.2 5.3 %fusion = f32[64,1,128]{2,1,0:T(1,128)S(1)} fusion(f32[64,128,1]{1,2,0:T(1,128)S(1)} %bitcast.124, f32[1,1,64,128,128]{4,3,2,1,0:T(8,128)} %param.17), kind=kOutput, calls=%fused_computation.7 | convolution fusion | flops 12582912 | bytes 4259840 | tf_op jit(solution)/shard_map/kij,ki->kj/dot_general | solution.py:83
  322.3 4.0 %all-to-all-start.6 = ((f32[8,24,128]{2,1,0:T(8,128)}), f32[8,24,128]{2,1,0:T(8,128)S(1)}, u32[]{:S(2)}, u32[]{:S(2)}) async-start(f32[8,24,128]{2,1,0:T(8,128)} %broadcast_in_dim.48), calls=%async_computation.6 | async-start | bytes 196608 | tf_op jit(solution)/shard_map/all_to_all | solution.py:16
  326.3 5.4 %all-to-all-done.6 = f32[8,24,128]{2,1,0:T(8,128)S(1)} async-done(((f32[8,24,128]{2,1,0:T(8,128)}), f32[8,24,128]{2,1,0:T(8,128)S(1)}, u32[]{:S(2)}, u32[]{:S(2)}) %all-to-all-start.6) | async-done | bytes 98336 | tf_op jit(solution)/shard_map/all_to_all | solution.py:16
  332.4 1.3 broadcast_in_dim.47
  333.7 7.5 %all-to-all-start.5 = ((f32[32,1,1]{2,1,0:T(1,128)}), f32[32,1,1]{2,1,0:T(1,128)S(1)}, u32[]{:S(2)}, u32[]{:S(2)}) async-start(f32[32,1,1]{2,1,0:T(1,128)} %broadcast_in_dim.47), calls=%async_computation.5 | async-start | bytes 32768 | tf_op jit(solution)/shard_map/all_to_all | solution.py:16
  341.2 9.3 %all-to-all-done.5 = f32[32,1,1]{2,1,0:T(1,128)S(1)} async-done(((f32[32,1,1]{2,1,0:T(1,128)}), f32[32,1,1]{2,1,0:T(1,128)S(1)}, u32[]{:S(2)}, u32[]{:S(2)}) %all-to-all-start.5) | async-done | bytes 160 | tf_op jit(solution)/shard_map/all_to_all | solution.py:16
  350.5 1.3 broadcast_in_dim.49
  351.7 4.1 %all-to-all-start.7 = ((f32[32,1,1]{2,1,0:T(1,128)}), f32[32,1,1]{2,1,0:T(1,128)S(1)}, u32[]{:S(2)}, u32[]{:S(2)}) async-start(f32[32,1,1]{2,1,0:T(1,128)} %broadcast_in_dim.49), calls=%async_computation.7 | async-start | bytes 32768 | tf_op jit(solution)/shard_map/all_to_all | solution.py:16
  356.5 8.8 %all-to-all-done.7 = f32[32,1,1]{2,1,0:T(1,128)S(1)} async-done(((f32[32,1,1]{2,1,0:T(1,128)}), f32[32,1,1]{2,1,0:T(1,128)S(1)}, u32[]{:S(2)}, u32[]{:S(2)}) %all-to-all-start.7) | async-done | bytes 160 | tf_op jit(solution)/shard_map/all_to_all | solution.py:16
  (71 shorter events, 17.8 us)
Async XLA Ops:
  7.2 34.5 %copy-start.5 = (s32[1,1,64]{2,1,0:T(1,128)S(1)}, s32[1,1,64]{2,1,0:T(1,128)}, u32[]{:S(2)}) copy-start(s32[1,1,64]{2,1,0:T(1,128)} %param.18) | copy-start | bytes 772
  7.2 101.4 %copy-start.1 = (f32[160,128]{1,0:T(8,128)S(1)}, f32[160,128]{1,0:T(8,128)}, u32[]{:S(2)}) copy-start(f32[160,128]{1,0:T(8,128)} %param.21) | copy-start | bytes 245764
  7.2 101.4 %copy-start = (f32[160,128]{1,0:T(8,128)S(1)}, f32[160,128]{1,0:T(8,128)}, u32[]{:S(2)}) copy-start(f32[160,128]{1,0:T(8,128)} %param.22) | copy-start | bytes 245764
  7.2 99.5 %all-gather.7.cloned.1.call-start = ((), (), s32[]{:S(2)}) async-start(), calls=%async_computation.8 | async-start | bytes 2703360 | tf_op jit(solution)/shard_map/all_gather | solution.py:11
  41.6 73.0 %copy-start.4 = (s32[1,1,64]{2,1,0:T(1,128)S(1)}, s32[1,1,64]{2,1,0:T(1,128)}, u32[]{:S(2)}) copy-start(s32[1,1,64]{2,1,0:T(1,128)} %param.19) | copy-start | bytes 772
  115.4 9.4 %all-to-all-start = ((f32[8,24,128]{2,1,0:T(8,128)}), f32[8,24,128]{2,1,0:T(8,128)S(1)}, u32[]{:S(2)}, u32[]{:S(2)}) async-start(f32[8,24,128]{2,1,0:T(8,128)} %broadcast_in_dim.42), calls=%async_computation | async-start | bytes 196608 | tf_op jit(solution)/shard_map/all_to_all | solution.py:16
  119.4 67.9 %all-gather.9.cloned.1.call-start = ((), (), s32[]{:S(2)}) async-start(), calls=%async_computation.9 | async-start | bytes 2703360 | tf_op jit(solution)/shard_map/all_gather | solution.py:11
  133.8 106.3 %copy-start.2 = (f32[160,128]{1,0:T(8,128)S(1)}, f32[160,128]{1,0:T(8,128)}, u32[]{:S(2)}) copy-start(f32[160,128]{1,0:T(8,128)} %param.24) | copy-start | bytes 245764
  133.8 106.3 %copy-start.3 = (f32[160,128]{1,0:T(8,128)S(1)}, f32[160,128]{1,0:T(8,128)}, u32[]{:S(2)}) copy-start(f32[160,128]{1,0:T(8,128)} %param.23) | copy-start | bytes 245764
  195.9 9.4 %all-to-all-start.2 = ((f32[8,24,128]{2,1,0:T(8,128)}), f32[8,24,128]{2,1,0:T(8,128)S(1)}, u32[]{:S(2)}, u32[]{:S(2)}) async-start(f32[8,24,128]{2,1,0:T(8,128)} %broadcast_in_dim.44), calls=%async_computation.2 | async-start | bytes 196608 | tf_op jit(solution)/shard_map/all_to_all | solution.py:16
  224.5 13.6 %all-to-all-start.3 = ((f32[32,1,1]{2,1,0:T(1,128)}), f32[32,1,1]{2,1,0:T(1,128)S(1)}, u32[]{:S(2)}, u32[]{:S(2)}) async-start(f32[32,1,1]{2,1,0:T(1,128)} %broadcast_in_dim.45), calls=%async_computation.3 | async-start | bytes 32768 | tf_op jit(solution)/shard_map/all_to_all | solution.py:16
  228.7 85.0 %all-gather.11.cloned.1.call-start = ((), (), s32[]{:S(2)}) async-start(), calls=%async_computation.10 | async-start | bytes 2703360 | tf_op jit(solution)/shard_map/all_gather | solution.py:11
  322.3 9.4 %all-to-all-start.6 = ((f32[8,24,128]{2,1,0:T(8,128)}), f32[8,24,128]{2,1,0:T(8,128)S(1)}, u32[]{:S(2)}, u32[]{:S(2)}) async-start(f32[8,24,128]{2,1,0:T(8,128)} %broadcast_in_dim.48), calls=%async_computation.6 | async-start | bytes 196608 | tf_op jit(solution)/shard_map/all_to_all | solution.py:16
  333.7 16.8 %all-to-all-start.5 = ((f32[32,1,1]{2,1,0:T(1,128)}), f32[32,1,1]{2,1,0:T(1,128)S(1)}, u32[]{:S(2)}, u32[]{:S(2)}) async-start(f32[32,1,1]{2,1,0:T(1,128)} %broadcast_in_dim.47), calls=%async_computation.5 | async-start | bytes 32768 | tf_op jit(solution)/shard_map/all_to_all | solution.py:16
  351.7 13.6 %all-to-all-start.7 = ((f32[32,1,1]{2,1,0:T(1,128)}), f32[32,1,1]{2,1,0:T(1,128)S(1)}, u32[]{:S(2)}, u32[]{:S(2)}) async-start(f32[32,1,1]{2,1,0:T(1,128)} %broadcast_in_dim.49), calls=%async_computation.7 | async-start | bytes 32768 | tf_op jit(solution)/shard_map/all_to_all | solution.py:16
Sparse Core Ops, SparseCore 0:
  42.6 64.0 all-gather.6
  134.7 52.4 all-gather.8
  264.0 49.5 all-gather.10
where the time goes:
time: 376 us; the launch traced here: 375 us
  waiting for transfers between devices  207 us (55%)
  matrix products  49.1 us (13%)
  blocking collectives  47.5 us (13%)
  starting transfers between devices  28 us (7%)
  between operations  18.6 us (5%)
  other arithmetic  13.1 us (3%)
  local copies, waits for them, and re-layouts  11.6 us (3%)
    all_gather x3, waiting for transfers between devices, total_of_pieces(): return lax.all_gather(array, axis).sum(0)  166 us
    all_to_all x6, waiting for transfers between devices, from_everyone(): return lax.all_to_all(copies, axis, split_axis=0, concat_axis=0, tiled=True)  41.4 us
    all_to_all x6, starting transfers between devices, from_everyone(): return lax.all_to_all(copies, axis, split_axis=0, concat_axis=0, tiled=True)  27.7 us
    dot_general x3, matrix products, forward_terms(): products = jnp.einsum('kij,kj->ki', flat_tiles, picked, precision=HIGH)  24.9 us
    all_to_all x2, blocking collectives, from_everyone(): return lax.all_to_all(copies, axis, split_axis=0, concat_axis=0, tiled=True)  24.4 us
    all_gather x1, blocking collectives, turned_gather(): out = lax.all_gather(both, axis, axis=0, tiled=True)  23 us
    dot_general x4, matrix products, apply_backward(): products = jnp.einsum('kij,ki->kj', flat_tiles, picked, precision=HIGH)  21.1 us
  transfers between devices with their start and end apart: 9, of which 9 were waited for; matrix products, arithmetic and copies ran while one was open for 0% of the time, Pallas kernels for 0%

commit v1 on v0

--- a/solution.py
+++ b/solution.py
@@ -25,7 +25,9 @@
     turned = [jnp.moveaxis(a, dim, 0) for a, dim in zip(arrays, dims)]
     widths = [t[0].size for t in turned]
     both = jnp.concatenate([t.reshape(-1, w) for t, w in zip(turned, widths)], axis=1)
-    out = lax.all_gather(both, axis, axis=0, tiled=True)
+    out = jnp.concatenate(
+        lax.all_to_all(jnp.stack([both] * lax.axis_size(axis)), axis, 0, 0), axis=0
+    )
     parts = jnp.split(out, [sum(widths[:k]) for k in range(1, len(widths))], axis=1)
     return tuple(
         (

time: 376 us -> 357 us (0.949)
  blocking collectives: 47.5 us -> 24.4 us
  starting transfers between devices: 28 us -> 34.2 us
    all_gather x1 -> x0, blocking collectives: 23 us -> none  [turned_gather(): out = lax.all_gather(both, axis, axis=0, tiled=True)]
    all_gather x3, waiting for transfers between devices: 166 us -> 159 us  [total_of_pieces(): return lax.all_gather(array, axis).sum(0)]
    all_to_all x0 -> x1, starting transfers between devices: none -> 6.19 us  [turned_gather(): lax.all_to_all(jnp.stack([both] * lax.axis_size(axis)), axis, 0, 0)]
    all_to_all x0 -> x1, waiting for transfers between devices: none -> 3.82 us  [turned_gather(): lax.all_to_all(jnp.stack([both] * lax.axis_size(axis)), axis, 0, 0)]
  transfers between devices with their start and end apart: 9 -> 10, of which waited for: 9 -> 10; matrix products, arithmetic and copies ran while one was open for 0% -> 1% of each run, Pallas kernels for 0% -> 0%
where the time goes in v1:
time: 357 us; the launch traced here: 356 us
  waiting for transfers between devices  205 us (57%)
  matrix products  49.1 us (14%)
  starting transfers between devices  34.2 us (10%)
  blocking collectives  24.4 us (7%)
  between operations  18.6 us (5%)
  other arithmetic  13.1 us (4%)
  local copies, waits for them, and re-layouts  12.2 us (3%)
    all_gather x3, waiting for transfers between devices, total_of_pieces(): return lax.all_gather(array, axis).sum(0)  159 us
    all_to_all x6, waiting for transfers between devices, from_everyone(): return lax.all_to_all(copies, axis, split_axis=0, concat_axis=0, tiled=True)  41.4 us
    all_to_all x6, starting transfers between devices, from_everyone(): return lax.all_to_all(copies, axis, split_axis=0, concat_axis=0, tiled=True)  27.7 us
    dot_general x3, matrix products, forward_terms(): products = jnp.einsum('kij,kj->ki', flat_tiles, picked, precision=HIGH)  24.9 us
    all_to_all x2, blocking collectives, from_everyone(): return lax.all_to_all(copies, axis, split_axis=0, concat_axis=0, tiled=True)  24.4 us
    dot_general x4, matrix products, apply_backward(): products = jnp.einsum('kij,ki->kj', flat_tiles, picked, precision=HIGH)  21.1 us
  transfers between devices with their start and end apart: 10, of which 10 were waited for; matrix products, arithmetic and copies ran while one was open for 1% of the time, Pallas kernels for 0%

profile of v1, /device:TPU:1, one launch (start us, length us, event | category | flops | bytes accessed | tf_op | source)
XLA Modules:
  0.0 356.3 jit_solution(8852839247714823892)
XLA Ops:
  8.7 6.2 %all-to-all-start = ((f32[8,16,72]{2,1,0:T(8,128)}), f32[8,16,72]{2,1,0:T(8,128)S(1)}, u32[]{:S(2)}, u32[]{:S(2)}) async-start(f32[8,16,72]{2,1,0:T(8,128)} %stack.2), calls=%async_computation | async-start | bytes 131072 | tf_op jit(solution)/shard_map/all_to_all | solution.py:29
  16.2 3.8 %all-to-all-done = f32[8,16,72]{2,1,0:T(8,128)S(1)} async-done(((f32[8,16,72]{2,1,0:T(8,128)}), f32[8,16,72]{2,1,0:T(8,128)S(1)}, u32[]{:S(2)}, u32[]{:S(2)}) %all-to-all-start) | async-done | bytes 36896 | tf_op jit(solution)/shard_map/all_to_all | solution.py:29
  20.9 8.3 %fusion.12 = f32[64,1,128]{2,1,0:T(1,128)S(1)} fusion(f32[64,128,1]{1,2,0:T(1,128)S(1)} %bitcast.127, f32[1,1,64,128,128]{4,3,2,1,0:T(8,128)} %param.17), kind=kOutput, calls=%fused_computation.19 | convolution fusion | flops 12582912 | bytes 4259840 | tf_op jit(solution)/shard_map/kij,kj->ki/dot_general | solution.py:76
  30.8 57.0 %all-gather.7.cloned.1.call-done = f32[5120,128]{1,0:T(8,128)} async-done(((f32[160,128]{1,0:T(8,128)}), f32[5120,128]{1,0:T(8,128)}) %all-gather.7.cloned.1.call-update) | async-done | bytes 2621456 | tf_op jit(solution)/shard_map/all_gather | solution.py:11
  87.8 1.9 reduce_sum.135
  90.4 5.3 %fusion.10 = f32[64,1,128]{2,1,0:T(1,128)S(1)} fusion(f32[64,128,1]{1,2,0:T(1,128)S(1)} %bitcast.128, f32[1,1,64,128,128]{4,3,2,1,0:T(8,128)} %param.17), kind=kOutput, calls=%fused_computation.17 | convolution fusion | flops 12582912 | bytes 4259840 | tf_op jit(solution)/shard_map/kij,ki->kj/dot_general | solution.py:85
  96.5 4.0 %all-to-all-start.1 = ((f32[8,24,128]{2,1,0:T(8,128)}), f32[8,24,128]{2,1,0:T(8,128)S(1)}, u32[]{:S(2)}, u32[]{:S(2)}) async-start(f32[8,24,128]{2,1,0:T(8,128)} %broadcast_in_dim.42), calls=%async_computation.1 | async-start | bytes 196608 | tf_op jit(solution)/shard_map/all_to_all | solution.py:16
  100.6 5.2 %all-to-all-done.1 = f32[8,24,128]{2,1,0:T(8,128)S(1)} async-done(((f32[8,24,128]{2,1,0:T(8,128)}), f32[8,24,128]{2,1,0:T(8,128)S(1)}, u32[]{:S(2)}, u32[]{:S(2)}) %all-to-all-start.1) | async-done | bytes 98336 | tf_op jit(solution)/shard_map/all_to_all | solution.py:16
  106.5 8.3 %fusion.8 = f32[64,1,128]{2,1,0:T(1,128)S(1)} fusion(f32[64,128,1]{1,2,0:T(1,128)S(1)} %bitcast.130, f32[1,1,64,128,128]{4,3,2,1,0:T(8,128)} %param.17), kind=kOutput, calls=%fused_computation.15 | convolution fusion | flops 12582912 | bytes 4259840 | tf_op jit(solution)/shard_map/kij,kj->ki/dot_general | solution.py:76
  115.7 52.7 %all-gather.9.cloned.1.call-done = f32[5120,128]{1,0:T(8,128)} async-done(((f32[160,128]{1,0:T(8,128)}), f32[5120,128]{1,0:T(8,128)}) %all-gather.9.cloned.1.call-update) | async-done | bytes 2621456 | tf_op jit(solution)/shard_map/all_gather | solution.py:11
  168.4 1.9 reduce_sum.139
  170.9 5.3 %fusion.6 = f32[64,1,128]{2,1,0:T(1,128)S(1)} fusion(f32[64,128,1]{1,2,0:T(1,128)S(1)} %bitcast.131, f32[1,1,64,128,128]{4,3,2,1,0:T(8,128)} %param.17), kind=kOutput, calls=%fused_computation.13 | convolution fusion | flops 12582912 | bytes 4259840 | tf_op jit(solution)/shard_map/kij,ki->kj/dot_general | solution.py:85
  177.0 4.0 %all-to-all-start.3 = ((f32[8,24,128]{2,1,0:T(8,128)}), f32[8,24,128]{2,1,0:T(8,128)S(1)}, u32[]{:S(2)}, u32[]{:S(2)}) async-start(f32[8,24,128]{2,1,0:T(8,128)} %broadcast_in_dim.44), calls=%async_computation.3 | async-start | bytes 196608 | tf_op jit(solution)/shard_map/all_to_all | solution.py:16
  181.6 4.7 %all-to-all-done.3 = f32[8,24,128]{2,1,0:T(8,128)S(1)} async-done(((f32[8,24,128]{2,1,0:T(8,128)}), f32[8,24,128]{2,1,0:T(8,128)S(1)}, u32[]{:S(2)}, u32[]{:S(2)}) %all-to-all-start.3) | async-done | bytes 98336 | tf_op jit(solution)/shard_map/all_to_all | solution.py:16
  187.6 16.7 %all_to_all.49 = f32[32,1,1]{2,1,0:T(1,128)S(1)} all-to-all(f32[32,1,1]{2,1,0:T(1,128)S(1)} %broadcast_in_dim.43), channel_id=1, replica_groups=mesh['row'=8,'col'=32] {'col'}, dimensions={0} | all-to-all | bytes 256 | tf_op jit(solution)/shard_map/all_to_all | solution.py:16
  204.3 1.3 broadcast_in_dim.45
  205.6 4.1 %all-to-all-start.4 = ((f32[32,1,1]{2,1,0:T(1,128)}), f32[32,1,1]{2,1,0:T(1,128)S(1)}, u32[]{:S(2)}, u32[]{:S(2)}) async-start(f32[32,1,1]{2,1,0:T(1,128)} %broadcast_in_dim.45), calls=%async_computation.4 | async-start | bytes 32768 | tf_op jit(solution)/shard_map/all_to_all | solution.py:16
  211.2 7.9 %all-to-all-done.4 = f32[32,1,1]{2,1,0:T(1,128)S(1)} async-done(((f32[32,1,1]{2,1,0:T(1,128)}), f32[32,1,1]{2,1,0:T(1,128)S(1)}, u32[]{:S(2)}, u32[]{:S(2)}) %all-to-all-start.4) | async-done | bytes 160 | tf_op jit(solution)/shard_map/all_to_all | solution.py:16
  221.9 5.3 %fusion.4 = f32[64,1,128]{2,1,0:T(1,128)S(1)} fusion(f32[64,128,1]{1,2,0:T(1,128)S(1)} %bitcast.133, f32[1,1,64,128,128]{4,3,2,1,0:T(8,128)} %param.17), kind=kOutput, calls=%fused_computation.11 | convolution fusion | flops 12582912 | bytes 4259840 | tf_op jit(solution)/shard_map/kij,ki->kj/dot_general | solution.py:85
  227.3 7.8 %all_to_all.50 = f32[8,24,128]{2,1,0:T(8,128)S(1)} all-to-all(f32[8,24,128]{2,1,0:T(8,128)S(1)} %broadcast_in_dim.46), channel_id=1, replica_groups=mesh['row'=8,'col'=32] {'row'}, dimensions={0} | all-to-all | bytes 196608 | tf_op jit(solution)/shard_map/all_to_all | solution.py:16
  235.8 8.3 %fusion.2 = f32[64,1,128]{2,1,0:T(1,128)S(1)} fusion(f32[64,128,1]{1,2,0:T(1,128)S(1)} %bitcast.125, f32[1,1,64,128,128]{4,3,2,1,0:T(8,128)} %param.17), kind=kOutput, calls=%fused_computation.9 | convolution fusion | flops 12582912 | bytes 4259840 | tf_op jit(solution)/shard_map/kij,kj->ki/dot_general | solution.py:76
  245.0 49.7 %all-gather.11.cloned.1.call-done = f32[5120,128]{1,0:T(8,128)} async-done(((f32[160,128]{1,0:T(8,128)}), f32[5120,128]{1,0:T(8,128)}) %all-gather.11.cloned.1.call-update) | async-done | bytes 2621456 | tf_op jit(solution)/shard_map/all_gather | solution.py:11
  294.7 1.9 reduce_sum.146
  297.3 5.3 %fusion = f32[64,1,128]{2,1,0:T(1,128)S(1)} fusion(f32[64,128,1]{1,2,0:T(1,128)S(1)} %bitcast.126, f32[1,1,64,128,128]{4,3,2,1,0:T(8,128)} %param.17), kind=kOutput, calls=%fused_computation.7 | convolution fusion | flops 12582912 | bytes 4259840 | tf_op jit(solution)/shard_map/kij,ki->kj/dot_general | solution.py:85
  303.4 4.0 %all-to-all-start.7 = ((f32[8,24,128]{2,1,0:T(8,128)}), f32[8,24,128]{2,1,0:T(8,128)S(1)}, u32[]{:S(2)}, u32[]{:S(2)}) async-start(f32[8,24,128]{2,1,0:T(8,128)} %broadcast_in_dim.48), calls=%async_computation.7 | async-start | bytes 196608 | tf_op jit(solution)/shard_map/all_to_all | solution.py:16
  307.3 5.4 %all-to-all-done.7 = f32[8,24,128]{2,1,0:T(8,128)S(1)} async-done(((f32[8,24,128]{2,1,0:T(8,128)}), f32[8,24,128]{2,1,0:T(8,128)S(1)}, u32[]{:S(2)}, u32[]{:S(2)}) %all-to-all-start.7) | async-done | bytes 98336 | tf_op jit(solution)/shard_map/all_to_all | solution.py:16
  313.4 1.3 broadcast_in_dim.47
  314.7 7.5 %all-to-all-start.6 = ((f32[32,1,1]{2,1,0:T(1,128)}), f32[32,1,1]{2,1,0:T(1,128)S(1)}, u32[]{:S(2)}, u32[]{:S(2)}) async-start(f32[32,1,1]{2,1,0:T(1,128)} %broadcast_in_dim.47), calls=%async_computation.6 | async-start | bytes 32768 | tf_op jit(solution)/shard_map/all_to_all | solution.py:16
  322.2 9.3 %all-to-all-done.6 = f32[32,1,1]{2,1,0:T(1,128)S(1)} async-done(((f32[32,1,1]{2,1,0:T(1,128)}), f32[32,1,1]{2,1,0:T(1,128)S(1)}, u32[]{:S(2)}, u32[]{:S(2)}) %all-to-all-start.6) | async-done | bytes 160 | tf_op jit(solution)/shard_map/all_to_all | solution.py:16
  331.5 1.3 broadcast_in_dim.49
  332.8 4.1 %all-to-all-start.8 = ((f32[32,1,1]{2,1,0:T(1,128)}), f32[32,1,1]{2,1,0:T(1,128)S(1)}, u32[]{:S(2)}, u32[]{:S(2)}) async-start(f32[32,1,1]{2,1,0:T(1,128)} %broadcast_in_dim.49), calls=%async_computation.8 | async-start | bytes 32768 | tf_op jit(solution)/shard_map/all_to_all | solution.py:16
  337.6 8.8 %all-to-all-done.8 = f32[32,1,1]{2,1,0:T(1,128)S(1)} async-done(((f32[32,1,1]{2,1,0:T(1,128)}), f32[32,1,1]{2,1,0:T(1,128)S(1)}, u32[]{:S(2)}, u32[]{:S(2)}) %all-to-all-start.8) | async-done | bytes 160 | tf_op jit(solution)/shard_map/all_to_all | solution.py:16
  (73 shorter events, 19.3 us)
Async XLA Ops:
  7.2 22.1 %copy-start.5 = (s32[1,1,64]{2,1,0:T(1,128)S(1)}, s32[1,1,64]{2,1,0:T(1,128)}, u32[]{:S(2)}) copy-start(s32[1,1,64]{2,1,0:T(1,128)} %param.18) | copy-start | bytes 772
  7.2 82.5 %copy-start.1 = (f32[160,128]{1,0:T(8,128)S(1)}, f32[160,128]{1,0:T(8,128)}, u32[]{:S(2)}) copy-start(f32[160,128]{1,0:T(8,128)} %param.21) | copy-start | bytes 245764
  7.2 82.5 %copy-start = (f32[160,128]{1,0:T(8,128)S(1)}, f32[160,128]{1,0:T(8,128)}, u32[]{:S(2)}) copy-start(f32[160,128]{1,0:T(8,128)} %param.22) | copy-start | bytes 245764
  8.7 11.4 %all-to-all-start = ((f32[8,16,72]{2,1,0:T(8,128)}), f32[8,16,72]{2,1,0:T(8,128)S(1)}, u32[]{:S(2)}, u32[]{:S(2)}) async-start(f32[8,16,72]{2,1,0:T(8,128)} %stack.2), calls=%async_computation | async-start | bytes 131072 | tf_op jit(solution)/shard_map/all_to_all | solution.py:29
  14.9 72.9 %all-gather.7.cloned.1.call-start = ((), (), s32[]{:S(2)}) async-start(), calls=%async_computation.9 | async-start | bytes 2703360 | tf_op jit(solution)/shard_map/all_gather | solution.py:11
  29.2 66.4 %copy-start.4 = (s32[1,1,64]{2,1,0:T(1,128)S(1)}, s32[1,1,64]{2,1,0:T(1,128)}, u32[]{:S(2)}) copy-start(s32[1,1,64]{2,1,0:T(1,128)} %param.19) | copy-start | bytes 772
  96.5 9.4 %all-to-all-start.1 = ((f32[8,24,128]{2,1,0:T(8,128)}), f32[8,24,128]{2,1,0:T(8,128)S(1)}, u32[]{:S(2)}, u32[]{:S(2)}) async-start(f32[8,24,128]{2,1,0:T(8,128)} %broadcast_in_dim.42), calls=%async_computation.1 | async-start | bytes 196608 | tf_op jit(solution)/shard_map/all_to_all | solution.py:16
  100.4 67.9 %all-gather.9.cloned.1.call-start = ((), (), s32[]{:S(2)}) async-start(), calls=%async_computation.10 | async-start | bytes 2703360 | tf_op jit(solution)/shard_map/all_gather | solution.py:11
  114.8 106.3 %copy-start.2 = (f32[160,128]{1,0:T(8,128)S(1)}, f32[160,128]{1,0:T(8,128)}, u32[]{:S(2)}) copy-start(f32[160,128]{1,0:T(8,128)} %param.24) | copy-start | bytes 245764
  114.8 106.3 %copy-start.3 = (f32[160,128]{1,0:T(8,128)S(1)}, f32[160,128]{1,0:T(8,128)}, u32[]{:S(2)}) copy-start(f32[160,128]{1,0:T(8,128)} %param.23) | copy-start | bytes 245764
  177.0 9.4 %all-to-all-start.3 = ((f32[8,24,128]{2,1,0:T(8,128)}), f32[8,24,128]{2,1,0:T(8,128)S(1)}, u32[]{:S(2)}, u32[]{:S(2)}) async-start(f32[8,24,128]{2,1,0:T(8,128)} %broadcast_in_dim.44), calls=%async_computation.3 | async-start | bytes 196608 | tf_op jit(solution)/shard_map/all_to_all | solution.py:16
  205.6 13.6 %all-to-all-start.4 = ((f32[32,1,1]{2,1,0:T(1,128)}), f32[32,1,1]{2,1,0:T(1,128)S(1)}, u32[]{:S(2)}, u32[]{:S(2)}) async-start(f32[32,1,1]{2,1,0:T(1,128)} %broadcast_in_dim.45), calls=%async_computation.4 | async-start | bytes 32768 | tf_op jit(solution)/shard_map/all_to_all | solution.py:16
  209.7 85.0 %all-gather.11.cloned.1.call-start = ((), (), s32[]{:S(2)}) async-start(), calls=%async_computation.11 | async-start | bytes 2703360 | tf_op jit(solution)/shard_map/all_gather | solution.py:11
  303.4 9.4 %all-to-all-start.7 = ((f32[8,24,128]{2,1,0:T(8,128)}), f32[8,24,128]{2,1,0:T(8,128)S(1)}, u32[]{:S(2)}, u32[]{:S(2)}) async-start(f32[8,24,128]{2,1,0:T(8,128)} %broadcast_in_dim.48), calls=%async_computation.7 | async-start | bytes 196608 | tf_op jit(solution)/shard_map/all_to_all | solution.py:16
  314.7 16.8 %all-to-all-start.6 = ((f32[32,1,1]{2,1,0:T(1,128)}), f32[32,1,1]{2,1,0:T(1,128)S(1)}, u32[]{:S(2)}, u32[]{:S(2)}) async-start(f32[32,1,1]{2,1,0:T(1,128)} %broadcast_in_dim.47), calls=%async_computation.6 | async-start | bytes 32768 | tf_op jit(solution)/shard_map/all_to_all | solution.py:16
  332.8 13.6 %all-to-all-start.8 = ((f32[32,1,1]{2,1,0:T(1,128)}), f32[32,1,1]{2,1,0:T(1,128)S(1)}, u32[]{:S(2)}, u32[]{:S(2)}) async-start(f32[32,1,1]{2,1,0:T(1,128)} %broadcast_in_dim.49), calls=%async_computation.8 | async-start | bytes 32768 | tf_op jit(solution)/shard_map/all_to_all | solution.py:16
Sparse Core Ops, SparseCore 0:
  30.2 57.5 all-gather.6
  115.8 52.4 all-gather.8
  245.1 49.5 all-gather.10
